TPU v7x, 32 devices: a whole 2x2x4 slice. The times are simulated.
32 devices in a mesh: grp: 2 (over y), row: 4 (over z), col: 4 (over x, core).
Axes of the slice: x: 2, y: 2, z: 4, core: 2. Of those that a mesh axis runs over, the one named last changes fastest.
Arguments:
- z_spectra: float32 [32, 2, 2, 4096], P(('grp', 'row', 'col')), parts along dimension 0, may hold values from -6 to 6
- n_spectra: float32 [32, 2, 2, 4096], P(('grp', 'col', 'row')), parts along dimension 0, may hold values from -6 to 6
- z_flags: int32 [32, 2], P(('grp', 'row', 'col')), parts along dimension 0, may hold values 0 or 1
- n_flags: int32 [32, 2], P(('grp', 'col', 'row')), parts along dimension 0, may hold values 0 or 1
- pair_mask: int32 [32, 16], P(('grp', 'row'), 'col'), parts along dimension 0, may hold values 0 or 1
Outputs:
- stacks: float32 [32, 16, 512], P(('grp', 'row'), 'col'), parts along dimension 0
There are 2 independent parts, one for each index of `grp`. A program takes and returns all parts, laid end to end along the dimension named above; each array names one. Nothing has to cross between parts.
All inputs are finite; a program needn't handle non-finite values. No bound on the sum of `z_flags` or of `n_flags` or of `pair_mask` on one device may be relied on, other than what follows from the above.
Results may differ from a plain program's by a relative error of at most 0.0037.
Values sent between devices are 32-bit elements; how exact they have to be, the bound alone decides.
A program may use at most 64 MiB of HBM per device.

v0:
```python
import math

import jax
import jax.numpy as jnp
from jax import lax
from jax.sharding import PartitionSpec as P

F = 4096
LAGS = 512
BANDS = 8


def lag_table(bin_count, total_bins, lag_count):
    freq_bins = jnp.arange(bin_count, dtype=jnp.int32)
    lag_steps = jnp.arange(lag_count, dtype=jnp.int32) - lag_count // 2
    phase_index = freq_bins[:, None] * lag_steps[None, :] % (2 * total_bins)
    angles = phase_index.astype(jnp.float32) * (math.pi / total_bins)
    weight = jnp.where(freq_bins == 0, 1.0, 2.0).astype(jnp.float32)[:, None]
    return jnp.concatenate([weight * jnp.cos(angles), -weight * jnp.sin(angles)], 0).astype(
        jnp.bfloat16
    )


def band_rows(full_table, first_bin, band_width, total_bins):
    real_rows = lax.dynamic_slice_in_dim(full_table, first_bin, band_width, 0)
    imag_rows = lax.dynamic_slice_in_dim(full_table, total_bins + first_bin, band_width, 0)
    return jnp.concatenate([real_rows, imag_rows], 0)


def correlate(row_spec, col_spec, lag_tab):
    z_real = row_spec[:, None, :, 0, :]
    z_imag = row_spec[:, None, :, 1, :]
    n_real = col_spec[None, :, :, 0, :]
    n_imag = col_spec[None, :, :, 1, :]
    real_part = z_real * n_real + z_imag * n_imag
    imag_part = z_imag * n_real - z_real * n_imag
    row_count, col_count, windows, bins = real_part.shape
    cross_spec = jnp.stack([real_part, imag_part], 3).astype(jnp.bfloat16)
    merged = cross_spec.reshape(row_count * col_count * windows, 2 * bins)
    product = jnp.dot(merged, lag_tab, preferred_element_type=jnp.float32)
    return product.reshape(row_count, col_count, windows, lag_tab.shape[1])


def stack_windows(corr, pair_marks):
    spread = jnp.sqrt(jnp.mean(corr * corr, -1, keepdims=True) + 1e-05)
    unit_corr = corr / spread
    window_count = jnp.maximum(jnp.sum(pair_marks, -1), 1.0)
    summed = jnp.sum(pair_marks[..., None] * unit_corr, -2)
    return summed / window_count[..., None]


def body(z_spectra, n_spectra, z_flags, n_flags, pair_mask):
    z_rows, z_marks = (
        lax.all_gather(z_spectra, "col", axis=0, tiled=True),
        lax.all_gather(z_flags.astype(jnp.float32), "col", axis=0, tiled=True),
    )
    n_marks = n_flags.astype(jnp.float32)
    row_count = z_rows.shape[0]
    windows = z_spectra.shape[1]
    band_width = F // BANDS
    full_table = lag_table(F, F, LAGS)
    col_spec = lax.all_gather(n_spectra, "row", axis=0, tiled=True)
    piece_marks = lax.all_gather(n_marks, "row", axis=0, tiled=True)

    def add_band(band_index, summed):
        first_bin = band_index * band_width
        lag_tab = band_rows(full_table, first_bin, band_width, F)
        z_band = lax.dynamic_slice_in_dim(z_rows, first_bin, band_width, 3)
        n_band = lax.dynamic_slice_in_dim(col_spec, first_bin, band_width, 3)
        return summed + correlate(z_band, n_band, lag_tab)

    initial = jnp.zeros((row_count, col_spec.shape[0], windows, LAGS), jnp.float32)
    corr = lax.fori_loop(0, BANDS, add_band, initial)
    running = corr
    joined = z_marks[:, None, :] * piece_marks[None, :, :]
    marks_now = joined
    state = (running, marks_now)
    running, marks_now = state
    stacked = stack_windows(running, marks_now)
    return stacked * pair_mask.astype(jnp.float32)[..., None]


def solution(mesh):
    placed = (
        P(("grp", "row", "col"), None, None, None),
        P(("grp", "col", "row"), None, None, None),
        P(("grp", "row", "col"), None),
        P(("grp", "col", "row"), None),
        P(("grp", "row"), "col"),
    )
    return jax.shard_map(
        body, mesh=mesh, in_specs=placed, out_specs=P(("grp", "row"), "col", None), check_vma=False
    )
```

profile of v0, /device:TPU:0, one launch (start us, length us, event | category | flops | bytes accessed | tf_op | source)
XLA Modules:
  0.0 99.7 jit_solution(9673217633503370301)
XLA Ops:
  0.0 36.3 %multiply_convert_fusion.1 = (bf16[4096,512]{1,0:T(8,128)(2,1)}, bf16[4096,512]{1,0:T(8,128)(2,1)}) fusion(s32[512]{0:T(512)S(1)} %iota_add_fusion, f32[4096]{0:T(1024)S(1)} %get-tuple-element.185, f32[4096]{0:T(1024)S(1)} %get-tuple-element.186), kind=kLoop, calls=%fused_computation.24 | loop fusion | flops 37748736 | bytes 8423424 | tf_op jit(solution)/shard_map/convert.2
  36.3 7.3 %pad_maximum_fusion.1 = bf16[8192,512]{1,0:T(8,128)(2,1)} fusion(bf16[4096,512]{1,0:T(8,128)(2,1)} %get-tuple-element.184, bf16[4096,512]{1,0:T(8,128)(2,1)} %get-tuple-element.183), kind=kLoop, calls=%fused_computation.22 | loop fusion | flops 16777216 | bytes 16777216 | tf_op jit(solution)/shard_map/concatenate | solution.py:19
  43.6 7.2 %all_gather.14 = f32[4,2,2,4096]{3,1,0,2:T(2,128)S(1)} all-gather(f32[1,2,2,4096]{3,1,0,2:T(2,128)S(1)} %copy.14), channel_id=1, replica_groups=mesh['grp'=2,'row'=4,'col'=4] {'col'}, dimensions={0}, use_global_device_ids=true | all-gather | bytes 327680 | tf_op jit(solution)/shard_map/all_gather | solution.py:54
  50.8 14.1 %all_gather.15 = f32[4,2,2,4096]{3,2,1,0:T(2,128)S(1)} all-gather(f32[1,2,2,4096]{3,2,1,0:T(2,128)S(1)} %copy-done), channel_id=1, replica_groups=mesh['grp'=2,'row'=4,'col'=4] {'row'}, dimensions={0}, use_global_device_ids=true | all-gather | bytes 327680 | tf_op jit(solution)/shard_map/all_gather | solution.py:62
  65.0 16.9 %while.16 = (s32[]{:T(128)}, f32[4,4,2,512]{3,1,2,0:T(4,128)S(1)}, f32[4,2,2,4096]{3,1,0,2:T(2,128)S(1)}, f32[4,2,2,4096]{3,2,1,0:T(2,128)S(1)}, bf16[8192,512]{...) while((s32[]{:T(128)}, f32[4,4,2,512]{3,1,2,0:T(4,128)S(1)}, ...), condition=%wide.region_1.2_spmd.clone, body=%wide.region_0.1_spmd.clone.sunk | while | flops 35946508 | bytes 3932428 | solution.py:73
  65.5 1.3 %constant_dynamic-slice_fusion.7 = (bf16[512,512]{1,0:T(8,128)(2,1)S(1)}, bf16[512,512]{1,0:T(8,128)(2,1)S(1)}) fusion(bf16[8192,512]{1,0:T(8,128)(2,1)} %get-tuple-element.266, s32[]{:T(128)S(6)} %select_n.74, s32[]{:T(128)S(6)} %select_n.75), kind=kLoop, calls=%fused_computation.13.clone.1 | loop fusion | bytes 2097160 | tf_op jit(solution)/shard_map/while/body/eval_jaxpr/dynamic_slice | solution.py:25
  66.8 0.3 convolution_add_fusion.2
  67.6 1.3 %constant_dynamic-slice_fusion.7 = (bf16[512,512]{1,0:T(8,128)(2,1)S(1)}, bf16[512,512]{1,0:T(8,128)(2,1)S(1)}) fusion(bf16[8192,512]{1,0:T(8,128)(2,1)} %get-tuple-element.266, s32[]{:T(128)S(6)} %select_n.74, s32[]{:T(128)S(6)} %select_n.75), kind=kLoop, calls=%fused_computation.13.clone.1 | loop fusion | bytes 2097160 | tf_op jit(solution)/shard_map/while/body/eval_jaxpr/dynamic_slice | solution.py:25
  68.9 0.3 convolution_add_fusion.2
  69.7 1.3 %constant_dynamic-slice_fusion.7 = (bf16[512,512]{1,0:T(8,128)(2,1)S(1)}, bf16[512,512]{1,0:T(8,128)(2,1)S(1)}) fusion(bf16[8192,512]{1,0:T(8,128)(2,1)} %get-tuple-element.266, s32[]{:T(128)S(6)} %select_n.74, s32[]{:T(128)S(6)} %select_n.75), kind=kLoop, calls=%fused_computation.13.clone.1 | loop fusion | bytes 2097160 | tf_op jit(solution)/shard_map/while/body/eval_jaxpr/dynamic_slice | solution.py:25
  71.0 0.3 convolution_add_fusion.2
  71.9 1.3 %constant_dynamic-slice_fusion.7 = (bf16[512,512]{1,0:T(8,128)(2,1)S(1)}, bf16[512,512]{1,0:T(8,128)(2,1)S(1)}) fusion(bf16[8192,512]{1,0:T(8,128)(2,1)} %get-tuple-element.266, s32[]{:T(128)S(6)} %select_n.74, s32[]{:T(128)S(6)} %select_n.75), kind=kLoop, calls=%fused_computation.13.clone.1 | loop fusion | bytes 2097160 | tf_op jit(solution)/shard_map/while/body/eval_jaxpr/dynamic_slice | solution.py:25
  73.1 0.3 convolution_add_fusion.2
  74.0 1.3 %constant_dynamic-slice_fusion.7 = (bf16[512,512]{1,0:T(8,128)(2,1)S(1)}, bf16[512,512]{1,0:T(8,128)(2,1)S(1)}) fusion(bf16[8192,512]{1,0:T(8,128)(2,1)} %get-tuple-element.266, s32[]{:T(128)S(6)} %select_n.74, s32[]{:T(128)S(6)} %select_n.75), kind=kLoop, calls=%fused_computation.13.clone.1 | loop fusion | bytes 2097160 | tf_op jit(solution)/shard_map/while/body/eval_jaxpr/dynamic_slice | solution.py:25
  75.3 0.3 convolution_add_fusion.2
  76.1 1.3 %constant_dynamic-slice_fusion.7 = (bf16[512,512]{1,0:T(8,128)(2,1)S(1)}, bf16[512,512]{1,0:T(8,128)(2,1)S(1)}) fusion(bf16[8192,512]{1,0:T(8,128)(2,1)} %get-tuple-element.266, s32[]{:T(128)S(6)} %select_n.74, s32[]{:T(128)S(6)} %select_n.75), kind=kLoop, calls=%fused_computation.13.clone.1 | loop fusion | bytes 2097160 | tf_op jit(solution)/shard_map/while/body/eval_jaxpr/dynamic_slice | solution.py:25
  77.4 0.3 convolution_add_fusion.2
  78.2 1.3 %constant_dynamic-slice_fusion.7 = (bf16[512,512]{1,0:T(8,128)(2,1)S(1)}, bf16[512,512]{1,0:T(8,128)(2,1)S(1)}) fusion(bf16[8192,512]{1,0:T(8,128)(2,1)} %get-tuple-element.266, s32[]{:T(128)S(6)} %select_n.74, s32[]{:T(128)S(6)} %select_n.75), kind=kLoop, calls=%fused_computation.13.clone.1 | loop fusion | bytes 2097160 | tf_op jit(solution)/shard_map/while/body/eval_jaxpr/dynamic_slice | solution.py:25
  79.5 0.3 convolution_add_fusion.2
  80.3 1.3 %constant_dynamic-slice_fusion.7 = (bf16[512,512]{1,0:T(8,128)(2,1)S(1)}, bf16[512,512]{1,0:T(8,128)(2,1)S(1)}) fusion(bf16[8192,512]{1,0:T(8,128)(2,1)} %get-tuple-element.266, s32[]{:T(128)S(6)} %select_n.74, s32[]{:T(128)S(6)} %select_n.75), kind=kLoop, calls=%fused_computation.13.clone.1 | loop fusion | bytes 2097160 | tf_op jit(solution)/shard_map/while/body/eval_jaxpr/dynamic_slice | solution.py:25
  81.6 0.3 convolution_add_fusion.2
  82.0 11.5 %all-gather.1 = f32[4,1,2]{2,1,0:T(1,128)S(1)} all-gather(f32[1,1,2]{2,1,0:T(1,128)S(1)} %convert_bitcast_fusion), channel_id=1, replica_groups=mesh['grp'=2,'row'=4,'col'=4] {'row'}, dimensions={0}, use_global_device_ids=true | all-gather | bytes 40 | tf_op jit(solution)/shard_map/all_gather | solution.py:63
  93.7 5.0 %all-gather = f32[4,1,2]{2,1,0:T(1,128)S(1)} all-gather(f32[1,1,2]{2,1,0:T(1,128)S(1)} %convert_bitcast_fusion.1), channel_id=1, replica_groups=mesh['grp'=2,'row'=4,'col'=4] {'col'}, dimensions={0}, use_global_device_ids=true | all-gather | bytes 40 | tf_op jit(solution)/shard_map/all_gather | solution.py:55
  99.0 0.7 divide_multiply_fusion
  (71 shorter events, 4.2 us)
Async XLA Ops:
  36.3 7.3 %copy-start.1 = (f32[1,2,2,4096]{3,2,1,0:T(2,128)S(1)}, f32[1,2,2,4096]{3,2,1,0:T(2,128)}, u32[]{:S(2)}) copy-start(f32[1,2,2,4096]{3,2,1,0:T(2,128)} %param.7) | copy-start | bytes 196612
  36.3 14.6 %copy-start = (f32[1,2,2,4096]{3,2,1,0:T(2,128)S(1)}, f32[1,2,2,4096]{3,2,1,0:T(2,128)}, u32[]{:S(2)}) copy-start(f32[1,2,2,4096]{3,2,1,0:T(2,128)} %param.8) | copy-start | bytes 196612
  65.0 17.1 %copy-start.3 = (s32[1,2]{1,0:T(1,128)S(1)}, s32[1,2]{1,0:T(1,128)}, u32[]{:S(2)}) copy-start(s32[1,2]{1,0:T(1,128)} %param.10) | copy-start | bytes 28
  65.0 28.7 %copy-start.4 = (s32[1,2]{1,0:T(1,128)S(1)}, s32[1,2]{1,0:T(1,128)}, u32[]{:S(2)}) copy-start(s32[1,2]{1,0:T(1,128)} %param.9) | copy-start | bytes 28
  65.0 34.0 %copy-start.2 = (s32[4,4]{1,0:T(4,128)S(1)}, s32[4,4]{1,0:T(4,128)}, u32[]{:S(2)}) copy-start(s32[4,4]{1,0:T(4,128)} %param.11) | copy-start | bytes 196
where the time goes:
time: 100 us; the launch traced here: 99.7 us
  other arithmetic  46.8 us (47%)
  blocking collectives  37.9 us (38%)
  local copies, waits for them, and re-layouts  11.8 us (12%)
  matrix products  2.23 us (2%)
    another operation x9, other arithmetic  37.4 us
    all_gather x1, blocking collectives, body(): col_spec = lax.all_gather(n_spectra, 'row', axis=0, tiled=True)  14.1 us
    all_gather x1, blocking collectives, body(): piece_marks = lax.all_gather(n_marks, 'row', axis=0, tiled=True)  11.5 us
    dynamic_slice x8, local copies, waits for them, and re-layouts, band_rows(): real_rows = lax.dynamic_slice_in_dim(full_table, first_bin, band_width, 0)  10.2 us
    concatenate x1, other arithmetic, lag_table(): jnp.concatenate([weight * jnp.cos(angles), -weight * jnp.sin(angles)], 0)  7.26 us
    all_gather x1, blocking collectives, body(): lax.all_gather(z_spectra, 'col', axis=0, tiled=True)  7.23 us
    all_gather x1, blocking collectives, body(): lax.all_gather(z_flags.astype(jnp.float32), 'col', axis=0, tiled=True)  5.05 us
    dot_general x8, matrix products, correlate(): product = jnp.dot(merged, lag_tab, preferred_element_type=jnp.float32)  2.23 us

commit v1 on v0

v1 whole, which is shorter than its diff:
```python
import functools
import math

import jax
import jax.numpy as jnp
import numpy as np
from jax import lax
from jax.experimental import pallas as pl
from jax.experimental.pallas import tpu as pltpu
from jax.sharding import PartitionSpec as P

LAGS = 512
LANES = 128
MESH = pl.DeviceIdType.MESH


def tables(bins):
    rows, blocks = bins // LANES, LAGS // LANES
    period = 2 * rows
    kt, short = np.arange(rows), np.arange(period)
    phi = 2 * np.pi * ((short[:, None] * kt[None, :]) % period) / period
    inner = np.block([[np.cos(phi), -np.sin(phi)], [np.sin(phi), np.cos(phi)]])
    lane, t0 = np.arange(LANES), np.arange(LANES)
    psi = np.pi * (t0[:, None] * lane[None, :]) / bins
    turn = np.stack([np.cos(psi), np.sin(psi)]).astype(np.float32)
    hop = np.arange(blocks) - blocks // 2
    chi = np.pi * ((LANES * hop[:, None] * lane[None, :]) % (2 * bins)) / bins
    outer = np.concatenate([np.cos(chi), -np.sin(chi)], 1).astype(np.float32)
    high = outer.astype(jnp.bfloat16)
    low = (outer - high.astype(np.float32)).astype(jnp.bfloat16)
    return inner.astype(jnp.bfloat16), turn, np.concatenate([high, low], 0)


def kernel(R, C, z_hbm, n_hbm, zf_hbm, nf_hbm, mask_hbm, inner_hbm, turn_hbm, outer_hbm, out_ref,
           z_buf, n_buf, zf_buf, nf_buf, mask_buf, inner, turn, outer,
           load_sem, z_send, z_recv, zf_send, zf_recv, right_send, left_send, n_recv,
           rf_send, lf_send, nf_recv):
    row, col = lax.axis_index("row"), lax.axis_index("col")
    W = z_buf.shape[1]
    bin_rows = z_buf.shape[2] // 2
    period = inner.shape[0] // 2
    blocks = outer.shape[0] // 2

    loads = [
        pltpu.make_async_copy(n_hbm.at[0], n_buf.at[row], load_sem.at[0]),
        pltpu.make_async_copy(z_hbm.at[0], z_buf.at[col], load_sem.at[1]),
        pltpu.make_async_copy(nf_hbm, nf_buf.at[row], load_sem.at[2]),
        pltpu.make_async_copy(zf_hbm, zf_buf.at[col], load_sem.at[3]),
        pltpu.make_async_copy(mask_hbm, mask_buf, load_sem.at[4]),
        pltpu.make_async_copy(inner_hbm, inner, load_sem.at[5]),
        pltpu.make_async_copy(turn_hbm, turn, load_sem.at[6]),
        pltpu.make_async_copy(outer_hbm, outer, load_sem.at[7]),
    ]
    for load in loads:
        load.start()

    has_left, has_right = row > 0, row < R - 1

    barrier = pltpu.get_barrier_semaphore()

    @pl.when(has_left)
    def _():
        pl.semaphore_signal(barrier, inc=1, device_id={"row": row - 1}, device_id_type=MESH)

    @pl.when(has_right)
    def _():
        pl.semaphore_signal(barrier, inc=1, device_id={"row": row + 1}, device_id_type=MESH)

    for step in range(1, C):
        pl.semaphore_signal(barrier, inc=1, device_id={"col": lax.rem(col + step, C)}, device_id_type=MESH)
    greeted = C - 1 + jnp.where(has_left, 1, 0) + jnp.where(has_right, 1, 0)
    pl.semaphore_wait(barrier, greeted)

    def spectrum(owner, w, send, to):
        return pltpu.make_async_remote_copy(
            n_buf.at[owner, w], n_buf.at[owner, w], send.at[owner, w], n_recv.at[owner, w],
            device_id={"row": to}, device_id_type=MESH)

    def flag(owner, send, to):
        return pltpu.make_async_remote_copy(
            nf_buf.at[owner], nf_buf.at[owner], send.at[owner], nf_recv.at[owner],
            device_id={"row": to}, device_id_type=MESH)

    def z_copy(owner, w, to):
        return pltpu.make_async_remote_copy(
            z_buf.at[owner, w], z_buf.at[owner, w], z_send.at[to, w], z_recv.at[owner, w],
            device_id={"col": to}, device_id_type=MESH)

    def zf_copy(owner, to):
        return pltpu.make_async_remote_copy(
            zf_buf.at[owner], zf_buf.at[owner], zf_send.at[to], zf_recv.at[owner],
            device_id={"col": to}, device_id_type=MESH)

    loads[2].wait()
    loads[0].wait()

    @pl.when(has_right)
    def _():
        flag(row, rf_send, row + 1).start()
        for w in range(W):
            spectrum(row, w, right_send, row + 1).start()

    @pl.when(has_left)
    def _():
        flag(row, lf_send, row - 1).start()
        for w in range(W):
            spectrum(row, w, left_send, row - 1).start()

    loads[3].wait()
    loads[1].wait()
    for step in range(1, C):
        zf_copy(col, lax.rem(col + step, C)).start()
    for w in range(W):
        for step in range(1, C):
            z_copy(col, w, lax.rem(col + step, C)).start()
    for load in loads[4:]:
        load.wait()

    spot = lax.broadcasted_iota(jnp.int32, (bin_rows, LANES), 0) + lax.broadcasted_iota(
        jnp.int32, (bin_rows, LANES), 1)
    weight = jnp.where(spot == 0, 1.0, 2.0).astype(jnp.float32)

    def unit(owner, w):
        n_real = n_buf[owner, w, pl.ds(0, bin_rows, stride=2), :] * weight
        n_imag = n_buf[owner, w, pl.ds(1, bin_rows, stride=2), :] * weight
        cross = []
        for i in range(C):
            z_real = z_buf[i, w, pl.ds(0, bin_rows, stride=2), :]
            z_imag = z_buf[i, w, pl.ds(1, bin_rows, stride=2), :]
            cross.append(jnp.concatenate(
                [z_real * n_real + z_imag * n_imag, z_imag * n_real - z_real * n_imag], 0
            ).astype(jnp.bfloat16))
        short = jnp.dot(inner[...], jnp.concatenate(cross, 1), preferred_element_type=jnp.float32)
        turned = []
        for i in range(C):
            real = short[:period, i * LANES:(i + 1) * LANES]
            imag = short[period:, i * LANES:(i + 1) * LANES]
            for part in range(LANES // period):
                cosine = turn[0, part * period:(part + 1) * period, :]
                sine = turn[1, part * period:(part + 1) * period, :]
                turned.append(jnp.concatenate(
                    [real * cosine - imag * sine, real * sine + imag * cosine], 1).astype(jnp.bfloat16))
        lags = lax.dot_general(outer[...], jnp.concatenate(turned, 0), (((1,), (1,)), ((), ())),
                               preferred_element_type=jnp.float32)
        lags = lags[:blocks] + lags[blocks:]
        n_flag = nf_buf[owner].astype(jnp.float32)
        mask = mask_buf[...].astype(jnp.float32)
        here = lax.broadcasted_iota(jnp.int32, mask.shape, 1) == owner
        kept = jnp.sum(jnp.where(here, mask, 0.0), axis=1, keepdims=True)
        for i in range(C):
            corr = lags[:, i * LANES:(i + 1) * LANES]
            marks = zf_buf[i].astype(jnp.float32) * n_flag
            count = jnp.maximum(jnp.sum(marks, axis=1, keepdims=True), 1.0)
            power = jnp.sum(jnp.sum(corr * corr, axis=0, keepdims=True), axis=1, keepdims=True)
            spread = jnp.sqrt(power / LAGS + 1e-05)
            gain = marks[:, w:w + 1] * kept[i:i + 1] / (count * spread)
            place = pl.ds(i * blocks * R + owner, blocks, stride=R)
            if w == 0:
                out_ref[place, :] = corr * gain
            else:
                out_ref[place, :] += corr * gain

    def arrive(owner, w, forward, send, f_send, to):
        if w == 0:
            flag(owner, f_send, to).wait_recv()
        spectrum(owner, w, send, to).wait_recv()

        @pl.when(forward)
        def _():
            if w == 0:
                flag(owner, f_send, to).start()
            spectrum(owner, w, send, to).start()

    def collect(step):
        for w in range(W):
            @pl.when(row - step >= 0)
            def _():
                arrive(row - step, w, has_right, right_send, rf_send, lax.rem(row + 1, R))

            @pl.when(row + step < R)
            def _():
                arrive(row + step, w, has_left, left_send, lf_send, lax.rem(row + R - 1, R))

    def compute(step):
        @pl.when(row - step >= 0)
        def _():
            for w in range(W):
                unit(row - step, w)

        @pl.when(row + step < R)
        def _():
            for w in range(W):
                unit(row + step, w)

    collect(1)
    for step in range(1, C):
        zf_copy(lax.rem(col + C - step, C), lax.rem(col + step, C)).wait_recv()
    for w in range(W):
        for step in range(1, C):
            z_copy(lax.rem(col + C - step, C), w, lax.rem(col + step, C)).wait_recv()
        unit(row, w)

    @pl.loop(2, R)
    def _(step):
        collect(step)
        compute(step - 1)

    compute(R - 1)

    for step in range(1, C):
        zf_copy(col, lax.rem(col + step, C)).wait_send()
        for w in range(W):
            z_copy(col, w, lax.rem(col + step, C)).wait_send()

    @pl.loop(0, R)
    def _(owner):
        @pl.when(has_right & (owner <= row))
        def _():
            flag(owner, rf_send, lax.rem(row + 1, R)).wait_send()
            for w in range(W):
                spectrum(owner, w, right_send, lax.rem(row + 1, R)).wait_send()

        @pl.when(has_left & (owner >= row))
        def _():
            flag(owner, lf_send, lax.rem(row + R - 1, R)).wait_send()
            for w in range(W):
                spectrum(owner, w, left_send, lax.rem(row + R - 1, R)).wait_send()


def body(R, C, z_spectra, n_spectra, z_flags, n_flags, pair_mask):
    windows, bins = z_spectra.shape[1], z_spectra.shape[3]
    rows, blocks = bins // LANES, LAGS // LANES
    inner, turn, outer = tables(bins)

    def interleave(x):
        return x.reshape(1, windows, 2, rows, LANES).transpose(0, 1, 3, 2, 4).reshape(
            1, windows, 2 * rows, LANES)

    DMA = pltpu.SemaphoreType.DMA
    out = pl.pallas_call(
        functools.partial(kernel, R, C),
        out_shape=jax.ShapeDtypeStruct((C * blocks * R, LANES), jnp.float32),
        in_specs=[pl.BlockSpec(memory_space=pl.ANY)] * 8,
        out_specs=pl.BlockSpec(memory_space=pltpu.VMEM),
        scratch_shapes=[
            pltpu.VMEM((C, windows, 2 * rows, LANES), jnp.float32),
            pltpu.VMEM((R, windows, 2 * rows, LANES), jnp.float32),
            pltpu.VMEM((C, 1, windows), jnp.int32),
            pltpu.VMEM((R, 1, windows), jnp.int32),
            pltpu.VMEM(pair_mask.shape, jnp.int32),
            pltpu.VMEM(inner.shape, jnp.bfloat16),
            pltpu.VMEM(turn.shape, jnp.float32),
            pltpu.VMEM(outer.shape, jnp.bfloat16),
            DMA((8,)),
            DMA((C, windows)), DMA((C, windows)), DMA((C,)), DMA((C,)),
            DMA((R, windows)), DMA((R, windows)), DMA((R, windows)),
            DMA((R,)), DMA((R,)), DMA((R,)),
        ],
        compiler_params=pltpu.CompilerParams(collective_id=0, has_side_effects=True),
        name="correlate",
    )(interleave(z_spectra), interleave(n_spectra), z_flags, n_flags, pair_mask,
      jnp.asarray(inner), jnp.asarray(turn), jnp.asarray(outer))
    return out.reshape(C, blocks, R, LANES).transpose(0, 2, 1, 3).reshape(C, R, LAGS)


def solution(mesh):
    placed = (
        P(("grp", "row", "col"), None, None, None),
        P(("grp", "col", "row"), None, None, None),
        P(("grp", "row", "col"), None),
        P(("grp", "col", "row"), None),
        P(("grp", "row"), "col"),
    )
    return jax.shard_map(
        functools.partial(body, mesh.shape["row"], mesh.shape["col"]), mesh=mesh,
        in_specs=placed, out_specs=P(("grp", "row"), "col", None), check_vma=False,
    )
```

time: 100 us -> 18.4 us (0.18)
  other arithmetic: 46.8 us -> 0 us
  blocking collectives: 37.9 us -> 0 us
  Pallas kernels: 0 us -> 16.8 us
  local copies, waits for them, and re-layouts: 11.8 us -> 1.38 us
  matrix products: 2.23 us -> 0 us
    another operation x17 -> x0, other arithmetic: 38.6 us -> none
    all_gather x4 -> x0, blocking collectives: 37.9 us -> none  [the longest x1 14.1 us: body(): col_spec = lax.all_gather(n_spectra, 'row', axis=0, tiled=True)]
    pallas_call x0 -> x1, Pallas kernels: none -> 16.8 us  [body(): pl.pallas_call(functools.partial(kernel, R, C), out_shape=jax.ShapeDtypeS...]
    dynamic_slice x8 -> x0, local copies, waits for them, and re-layouts: 10.2 us -> none  [band_rows(): real_rows = lax.dynamic_slice_in_dim(full_table, first_bin, band_width, 0)]
    concatenate x1 -> x0, other arithmetic: 7.26 us -> none  [lag_table(): jnp.concatenate([weight * jnp.cos(angles), -weight * jnp.sin(angles)], 0)]
    dot_general x8 -> x0, matrix products: 2.23 us -> none  [correlate(): product = jnp.dot(merged, lag_tab, preferred_element_type=jnp.float32)]
    unnamed x11 -> x1, local copies, waits for them, and re-layouts: 0.07 us -> 1.38 us
where the time goes in v1:
time: 18.4 us; the launch traced here: 18.2 us
  Pallas kernels  16.8 us (91%)
  local copies, waits for them, and re-layouts  1.38 us (8%)
    pallas_call x1, Pallas kernels, body(): pl.pallas_call(functools.partial(kernel, R, C), out_shape=jax.ShapeDtypeS...  16.8 us
    unnamed x1, local copies, waits for them, and re-layouts  1.38 us

profile of v1, /device:TPU:0, one launch (start us, length us, event | category | flops | bytes accessed | tf_op | source)
XLA Modules:
  0.0 18.2 jit_solution(8137097762372471685)
XLA Ops:
  0.0 16.8 %correlate.1 = f32[64,128]{1,0:T(8,128)} custom-call(f32[1,2,64,128]{3,2,1,0:T(8,128)} %bitcast.16, f32[1,2,64,128]{3,2,1,0:T(8,128)} %bitcast.17, s32[1,2]{1,0:T(1,128)} %zf_hbm.1, s32[1,2]{1,0:T(1,128)} %nf_hbm.1, s32[4,4]{1,0:T(4,128)} %mask_hbm.1, bf16[128,64]{1,0:T(8,128)(2,1)} %constant.6.clone.inner_hbm, f32[2,128,128]{2,1,0:T(8,128)} %constant.7.clone.turn_hbm, ...), custom_call_target="tpu_custom_call" | custom-call | tf_op jit(solution)/shard_map/correlate/pallas_call | solution.py:240
  16.9 1.4 %copy.13 = f32[4,4,512]{2,1,0:T(4,128)} copy(f32[4,4,512]{2,1,0:T(4,128)} %bitcast.15) | data formatting | bytes 65536

commit v2 on v1

--- a/solution.py
+++ b/solution.py
@@ -12,6 +12,7 @@
 LAGS = 512
 LANES = 128
 MESH = pl.DeviceIdType.MESH
+REACH = 3
 
 
 def tables(bins):
@@ -31,10 +32,10 @@
     return inner.astype(jnp.bfloat16), turn, np.concatenate([high, low], 0)
 
 
-def kernel(R, C, z_hbm, n_hbm, zf_hbm, nf_hbm, mask_hbm, inner_hbm, turn_hbm, outer_hbm, out_ref,
+def kernel(R, C, reach, z_hbm, n_hbm, zf_hbm, nf_hbm, mask_hbm, inner_hbm, turn_hbm, outer_hbm, out_ref,
            z_buf, n_buf, zf_buf, nf_buf, mask_buf, inner, turn, outer,
            load_sem, z_send, z_recv, zf_send, zf_recv, right_send, left_send, n_recv,
-           rf_send, lf_send, nf_recv):
+           rf_send, lf_send, nf_recv, own_send, own_f_send, ready):
     row, col = lax.axis_index("row"), lax.axis_index("col")
     W = z_buf.shape[1]
     bin_rows = z_buf.shape[2] // 2
@@ -55,21 +56,36 @@
         load.start()
 
     has_left, has_right = row > 0, row < R - 1
-
     barrier = pltpu.get_barrier_semaphore()
 
-    @pl.when(has_left)
-    def _():
-        pl.semaphore_signal(barrier, inc=1, device_id={"row": row - 1}, device_id_type=MESH)
-
-    @pl.when(has_right)
-    def _():
-        pl.semaphore_signal(barrier, inc=1, device_id={"row": row + 1}, device_id_type=MESH)
+    def there(hop):
+        return (row + hop < R) if hop > 0 else (row + hop >= 0)
+
+    for hop in (-1, 1):
+        @pl.when(there(hop))
+        def _():
+            pl.semaphore_signal(barrier, inc=1, device_id={"row": row + hop}, device_id_type=MESH)
 
     for step in range(1, C):
         pl.semaphore_signal(barrier, inc=1, device_id={"col": lax.rem(col + step, C)}, device_id_type=MESH)
-    greeted = C - 1 + jnp.where(has_left, 1, 0) + jnp.where(has_right, 1, 0)
-    pl.semaphore_wait(barrier, greeted)
+    pl.semaphore_wait(barrier, C - 1 + jnp.where(has_left, 1, 0) + jnp.where(has_right, 1, 0))
+
+    def tell(hop):
+        far = abs(hop) + 1
+        back = -1 if hop > 0 else 1
+        if far <= reach:
+            @pl.when(there(hop) & there(back))
+            def _():
+                pl.semaphore_signal(ready.at[int(hop < 0), far], inc=1,
+                                    device_id={"row": row + back}, device_id_type=MESH)
+
+    def learn(hop):
+        @pl.when(there(hop))
+        def _():
+            pl.semaphore_wait(ready.at[int(hop < 0), abs(hop)], 1)
+
+    tell(1)
+    tell(-1)
 
     def spectrum(owner, w, send, to):
         return pltpu.make_async_remote_copy(
@@ -91,21 +107,33 @@
             zf_buf.at[owner], zf_buf.at[owner], zf_send.at[to], zf_recv.at[owner],
             device_id={"col": to}, device_id_type=MESH)
 
+    def own_copy(hop, w):
+        side, far = int(hop < 0), abs(hop) - 1
+        return pltpu.make_async_remote_copy(
+            n_buf.at[row, w], n_buf.at[row, w], own_send.at[side, far, w], n_recv.at[row, w],
+            device_id={"row": row + hop}, device_id_type=MESH)
+
+    def own_flag(hop):
+        side, far = int(hop < 0), abs(hop) - 1
+        return pltpu.make_async_remote_copy(
+            nf_buf.at[row], nf_buf.at[row], own_f_send.at[side, far], nf_recv.at[row],
+            device_id={"row": row + hop}, device_id_type=MESH)
+
+    def send_own(hop):
+        @pl.when(there(hop))
+        def _():
+            own_flag(hop).start()
+            for w in range(W):
+                own_copy(hop, w).start()
+
+    for hop in range(2, reach + 1):
+        learn(-hop)
+        tell(-hop)
     loads[2].wait()
     loads[0].wait()
-
-    @pl.when(has_right)
-    def _():
-        flag(row, rf_send, row + 1).start()
-        for w in range(W):
-            spectrum(row, w, right_send, row + 1).start()
-
-    @pl.when(has_left)
-    def _():
-        flag(row, lf_send, row - 1).start()
-        for w in range(W):
-            spectrum(row, w, left_send, row - 1).start()
-
+    for hop in range(reach, 0, -1):
+        send_own(-hop)
+    send_own(1)
     loads[3].wait()
     loads[1].wait()
     for step in range(1, C):
@@ -113,6 +141,10 @@
     for w in range(W):
         for step in range(1, C):
             z_copy(col, w, lax.rem(col + step, C)).start()
+    for hop in range(2, reach + 1):
+        learn(hop)
+        tell(hop)
+        send_own(hop)
     for load in loads[4:]:
         load.wait()
 
@@ -120,21 +152,22 @@
         jnp.int32, (bin_rows, LANES), 1)
     weight = jnp.where(spot == 0, 1.0, 2.0).astype(jnp.float32)
 
-    def unit(owner, w):
-        n_real = n_buf[owner, w, pl.ds(0, bin_rows, stride=2), :] * weight
-        n_imag = n_buf[owner, w, pl.ds(1, bin_rows, stride=2), :] * weight
+    def unit(owner):
+        pairs = [(i, w) for i in range(C) for w in range(W)]
+        n_real = [n_buf[owner, w, pl.ds(0, bin_rows, stride=2), :] * weight for w in range(W)]
+        n_imag = [n_buf[owner, w, pl.ds(1, bin_rows, stride=2), :] * weight for w in range(W)]
         cross = []
-        for i in range(C):
+        for i, w in pairs:
             z_real = z_buf[i, w, pl.ds(0, bin_rows, stride=2), :]
             z_imag = z_buf[i, w, pl.ds(1, bin_rows, stride=2), :]
             cross.append(jnp.concatenate(
-                [z_real * n_real + z_imag * n_imag, z_imag * n_real - z_real * n_imag], 0
+                [z_real * n_real[w] + z_imag * n_imag[w], z_imag * n_real[w] - z_real * n_imag[w]], 0
             ).astype(jnp.bfloat16))
         short = jnp.dot(inner[...], jnp.concatenate(cross, 1), preferred_element_type=jnp.float32)
         turned = []
-        for i in range(C):
-            real = short[:period, i * LANES:(i + 1) * LANES]
-            imag = short[period:, i * LANES:(i + 1) * LANES]
+        for at in range(len(pairs)):
+            real = short[:period, at * LANES:(at + 1) * LANES]
+            imag = short[period:, at * LANES:(at + 1) * LANES]
             for part in range(LANES // period):
                 cosine = turn[0, part * period:(part + 1) * period, :]
                 sine = turn[1, part * period:(part + 1) * period, :]
@@ -148,22 +181,24 @@
         here = lax.broadcasted_iota(jnp.int32, mask.shape, 1) == owner
         kept = jnp.sum(jnp.where(here, mask, 0.0), axis=1, keepdims=True)
         for i in range(C):
-            corr = lags[:, i * LANES:(i + 1) * LANES]
             marks = zf_buf[i].astype(jnp.float32) * n_flag
             count = jnp.maximum(jnp.sum(marks, axis=1, keepdims=True), 1.0)
-            power = jnp.sum(jnp.sum(corr * corr, axis=0, keepdims=True), axis=1, keepdims=True)
-            spread = jnp.sqrt(power / LAGS + 1e-05)
-            gain = marks[:, w:w + 1] * kept[i:i + 1] / (count * spread)
-            place = pl.ds(i * blocks * R + owner, blocks, stride=R)
-            if w == 0:
-                out_ref[place, :] = corr * gain
-            else:
-                out_ref[place, :] += corr * gain
+            gain = marks * kept[i:i + 1] / count
+            total = jnp.zeros((blocks, LANES), jnp.float32)
+            for w in range(W):
+                at = i * W + w
+                corr = lags[:, at * LANES:(at + 1) * LANES]
+                power = jnp.sum(jnp.sum(corr * corr, axis=0, keepdims=True), axis=1, keepdims=True)
+                spread = jnp.sqrt(power / LAGS + 1e-05)
+                total = total + corr * (gain[:, w:w + 1] / spread)
+            out_ref[pl.ds(i * blocks * R + owner, blocks, stride=R), :] = total
 
     def arrive(owner, w, forward, send, f_send, to):
         if w == 0:
             flag(owner, f_send, to).wait_recv()
         spectrum(owner, w, send, to).wait_recv()
+        if forward is False:
+            return
 
         @pl.when(forward)
         def _():
@@ -171,56 +206,63 @@
                 flag(owner, f_send, to).start()
             spectrum(owner, w, send, to).start()
 
-    def collect(step):
-        for w in range(W):
-            @pl.when(row - step >= 0)
-            def _():
-                arrive(row - step, w, has_right, right_send, rf_send, lax.rem(row + 1, R))
-
-            @pl.when(row + step < R)
-            def _():
-                arrive(row + step, w, has_left, left_send, lf_send, lax.rem(row + R - 1, R))
-
-    def compute(step):
-        @pl.when(row - step >= 0)
-        def _():
-            for w in range(W):
-                unit(row - step, w)
-
-        @pl.when(row + step < R)
-        def _():
-            for w in range(W):
-                unit(row + step, w)
-
-    collect(1)
     for step in range(1, C):
         zf_copy(lax.rem(col + C - step, C), lax.rem(col + step, C)).wait_recv()
     for w in range(W):
         for step in range(1, C):
             z_copy(lax.rem(col + C - step, C), w, lax.rem(col + step, C)).wait_recv()
-        unit(row, w)
-
-    @pl.loop(2, R)
-    def _(step):
-        collect(step)
-        compute(step - 1)
-
-    compute(R - 1)
+    unit(row)
+
+    def take(p):
+        left = p <= row
+        owner = jnp.where(left, row - p, p)
+        if reach == R - 1:
+            for w in range(W):
+                arrive(owner, w, False, right_send, rf_send, lax.rem(row + 1, R))
+        else:
+            @pl.when(left)
+            def _():
+                for w in range(W):
+                    arrive(owner, w, has_right & (p >= reach), right_send, rf_send, lax.rem(row + 1, R))
+
+            @pl.when(p > row)
+            def _():
+                for w in range(W):
+                    arrive(owner, w, has_left & (p - row >= reach), left_send, lf_send,
+                           lax.rem(row + R - 1, R))
+        unit(owner)
+
+    if R <= 4:
+        for p in range(1, R):
+            take(p)
+    else:
+        pl.loop(1, R)(take)
+
+    hops = [sign * hop for hop in range(1, reach + 1) for sign in (1, -1)]
+    for hop in hops:
+        @pl.when(there(hop))
+        def _():
+            own_flag(hop).wait_send()
+            for w in range(W):
+                own_copy(hop, w).wait_send()
 
     for step in range(1, C):
         zf_copy(col, lax.rem(col + step, C)).wait_send()
         for w in range(W):
             z_copy(col, w, lax.rem(col + step, C)).wait_send()
 
+    if reach == R - 1:
+        return
+
     @pl.loop(0, R)
     def _(owner):
-        @pl.when(has_right & (owner <= row))
+        @pl.when(has_right & (owner <= row - reach))
         def _():
             flag(owner, rf_send, lax.rem(row + 1, R)).wait_send()
             for w in range(W):
                 spectrum(owner, w, right_send, lax.rem(row + 1, R)).wait_send()
 
-        @pl.when(has_left & (owner >= row))
+        @pl.when(has_left & (owner >= row + reach))
         def _():
             flag(owner, lf_send, lax.rem(row + R - 1, R)).wait_send()
             for w in range(W):
@@ -236,10 +278,11 @@
         return x.reshape(1, windows, 2, rows, LANES).transpose(0, 1, 3, 2, 4).reshape(
             1, windows, 2 * rows, LANES)
 
+    reach = min(REACH, R - 1)
     DMA = pltpu.SemaphoreType.DMA
     out = pl.pallas_call(
-        functools.partial(kernel, R, C),
-        out_shape=jax.ShapeDtypeStruct((C * blocks * R, LANES), jnp.float32),
+        functools.partial(kernel, R, C, reach),
+        out_shape=pltpu.VMEM((C * blocks * R, LANES), jnp.float32),
         in_specs=[pl.BlockSpec(memory_space=pl.ANY)] * 8,
         out_specs=pl.BlockSpec(memory_space=pltpu.VMEM),
         scratch_shapes=[
@@ -255,6 +298,7 @@
             DMA((C, windows)), DMA((C, windows)), DMA((C,)), DMA((C,)),
             DMA((R, windows)), DMA((R, windows)), DMA((R, windows)),
             DMA((R,)), DMA((R,)), DMA((R,)),
+            DMA((2, reach, windows)), DMA((2, reach)), pltpu.SemaphoreType.REGULAR((2, reach + 1)),
         ],
         compiler_params=pltpu.CompilerParams(collective_id=0, has_side_effects=True),
         name="correlate",

time: 18.4 us -> 14.7 us (0.80)
  Pallas kernels: 16.8 us -> 13.9 us
  local copies, waits for them, and re-layouts: 1.38 us -> 0.62 us
    pallas_call x1, Pallas kernels: 16.8 us -> 13.9 us  [body(): pl.pallas_call(functools.partial(kernel, R, C, reach), out_shape=pltpu.VM...]
    unnamed x1, local copies, waits for them, and re-layouts: 1.38 us -> 0.62 us
where the time goes in v2:
time: 14.7 us; the launch traced here: 14.6 us
  Pallas kernels  13.9 us (95%)
  local copies, waits for them, and re-layouts  0.62 us (4%)
    pallas_call x1, Pallas kernels, body(): pl.pallas_call(functools.partial(kernel, R, C, reach), out_shape=pltpu.VM...  13.9 us
    unnamed x1, local copies, waits for them, and re-layouts  0.62 us

profile of v2, /device:TPU:0, one launch (start us, length us, event | category | flops | bytes accessed | tf_op | source)
XLA Modules:
  0.0 14.6 jit_solution(1109530242377157439)
XLA Ops:
  0.0 13.9 %correlate.1 = f32[64,128]{1,0:T(8,128)S(1)} custom-call(f32[1,2,64,128]{3,2,1,0:T(8,128)} %bitcast.16, f32[1,2,64,128]{3,2,1,0:T(8,128)} %bitcast.17, s32[1,2]{1,0:T(1,128)} %zf_hbm.1, s32[1,2]{1,0:T(1,128)} %nf_hbm.1, s32[4,4]{1,0:T(4,128)} %mask_hbm.1, bf16[128,64]{1,0:T(8,128)(2,1)} %constant.6.clone.inner_hbm, f32[2,128,128]{2,1,0:T(8,128)} %constant.7.clone.turn_hbm, ...), custom_call_target="tpu_custom_call" | custom-call | tf_op jit(solution)/shard_map/correlate/pallas_call | solution.py:283
  13.9 0.6 %copy.13 = f32[4,4,512]{2,1,0:T(4,128)} copy(f32[4,4,512]{2,1,0:T(4,128)S(1)} %bitcast.15) | data formatting | bytes 65536

commit v3 on v2

--- a/solution.py
+++ b/solution.py
@@ -35,7 +35,7 @@
 def kernel(R, C, reach, z_hbm, n_hbm, zf_hbm, nf_hbm, mask_hbm, inner_hbm, turn_hbm, outer_hbm, out_ref,
            z_buf, n_buf, zf_buf, nf_buf, mask_buf, inner, turn, outer,
            load_sem, z_send, z_recv, zf_send, zf_recv, right_send, left_send, n_recv,
-           rf_send, lf_send, nf_recv, own_send, own_f_send, ready):
+           rf_send, lf_send, nf_recv, own_send, own_f_send, ready, turn_sem):
     row, col = lax.axis_index("row"), lax.axis_index("col")
     W = z_buf.shape[1]
     bin_rows = z_buf.shape[2] // 2
@@ -119,6 +119,9 @@
             nf_buf.at[row], nf_buf.at[row], own_f_send.at[side, far], nf_recv.at[row],
             device_id={"row": row + hop}, device_id_type=MESH)
 
+    pairs = C % 2 == 0
+    first = (lax.rem(col, 2) == 0) if pairs else (col >= 0)
+
     def send_own(hop):
         @pl.when(there(hop))
         def _():
@@ -131,8 +134,11 @@
         tell(-hop)
     loads[2].wait()
     loads[0].wait()
-    for hop in range(reach, 0, -1):
-        send_own(-hop)
+    @pl.when(first)
+    def _():
+        for hop in range(reach, 0, -1):
+            send_own(-hop)
+
     send_own(1)
     loads[3].wait()
     loads[1].wait()
@@ -141,6 +147,33 @@
     for w in range(W):
         for step in range(1, C):
             z_copy(col, w, lax.rem(col + step, C)).start()
+    @pl.when(first)
+    def _():
+        for hop in range(1, reach + 1):
+            @pl.when((row == hop) | ((row > hop) & (hop == reach)))
+            def _():
+                for w in range(W):
+                    own_copy(-hop, w).wait_send()
+
+        if pairs:
+            pl.semaphore_signal(turn_sem, inc=1, device_id={"col": lax.rem(col + 1, C)}, device_id_type=MESH)
+
+    @pl.when(jnp.logical_not(first))
+    def _():
+        send_own(-1)
+        held = row == R - 1
+
+        @pl.when(held)
+        def _():
+            pl.semaphore_wait(turn_sem, 1)
+
+        for hop in range(reach, 1, -1):
+            send_own(-hop)
+
+        @pl.when(jnp.logical_not(held))
+        def _():
+            pl.semaphore_wait(turn_sem, 1)
+
     for hop in range(2, reach + 1):
         learn(hop)
         tell(hop)
@@ -243,8 +276,16 @@
         @pl.when(there(hop))
         def _():
             own_flag(hop).wait_send()
-            for w in range(W):
-                own_copy(hop, w).wait_send()
+            if hop > 0:
+                for w in range(W):
+                    own_copy(hop, w).wait_send()
+            else:
+                waited = first & ((row == -hop) | ((row > -hop) & (-hop == reach)))
+
+                @pl.when(jnp.logical_not(waited))
+                def _():
+                    for w in range(W):
+                        own_copy(hop, w).wait_send()
 
     for step in range(1, C):
         zf_copy(col, lax.rem(col + step, C)).wait_send()
@@ -299,6 +340,7 @@
             DMA((R, windows)), DMA((R, windows)), DMA((R, windows)),
             DMA((R,)), DMA((R,)), DMA((R,)),
             DMA((2, reach, windows)), DMA((2, reach)), pltpu.SemaphoreType.REGULAR((2, reach + 1)),
+            pltpu.SemaphoreType.REGULAR,
         ],
         compiler_params=pltpu.CompilerParams(collective_id=0, has_side_effects=True),
         name="correlate",

time: 14.7 us -> 13.6 us (0.925)
  the two profiles are of different devices: /device:TPU:0 before, /device:TPU:1 now
where the time goes in v3:
time: 13.6 us; the launch traced here: 13.5 us
  Pallas kernels  12.9 us (95%)
  local copies, waits for them, and re-layouts  0.62 us (5%)
    pallas_call x1, Pallas kernels, body(): pl.pallas_call(functools.partial(kernel, R, C, reach), out_shape=pltpu.VM...  12.9 us
    unnamed x1, local copies, waits for them, and re-layouts  0.62 us

profile of v3, /device:TPU:1, one launch (start us, length us, event | category | flops | bytes accessed | tf_op | source)
XLA Modules:
  0.0 13.5 jit_solution(16198298582000661381)
XLA Ops:
  0.0 12.9 %correlate.1 = f32[64,128]{1,0:T(8,128)S(1)} custom-call(f32[1,2,64,128]{3,2,1,0:T(8,128)} %bitcast.16, f32[1,2,64,128]{3,2,1,0:T(8,128)} %bitcast.17, s32[1,2]{1,0:T(1,128)} %zf_hbm.1, s32[1,2]{1,0:T(1,128)} %nf_hbm.1, s32[4,4]{1,0:T(4,128)} %mask_hbm.1, bf16[128,64]{1,0:T(8,128)(2,1)} %constant.6.clone.inner_hbm, f32[2,128,128]{2,1,0:T(8,128)} %constant.7.clone.turn_hbm, ...), custom_call_target="tpu_custom_call" | custom-call | tf_op jit(solution)/shard_map/correlate/pallas_call | solution.py:324
  12.9 0.6 %copy.13 = f32[4,4,512]{2,1,0:T(4,128)} copy(f32[4,4,512]{2,1,0:T(4,128)S(1)} %bitcast.15) | data formatting | bytes 65536
